TPU v7x, 512 devices: a whole 4x4x16 slice. The times are simulated.
512 devices in a mesh: ma: 64 (over z_lo, x, core), af: 8 (over y, z_hi).
Axes of the slice: x: 4, y: 4, z: 16 (z_hi: 2, z_lo: 8; z = z_hi * 8 + z_lo), core: 2. Of those that a mesh axis runs over, the one named last changes fastest.
Arguments:
- coeffs: bfloat16 [512, 512, 2049], P('ma', 'af'), parts along dimension 1, may hold values from -6 to 6
- legendre: bfloat16 [512, 256, 2049], P('ma'), may hold values from -0.1875 to 0.1875
- assign: int32 [512], P('ma'), may hold values from 0 to 511, each once
Outputs:
- fourier: float32 [512, 512, 1024], P('ma', 'af'), parts along dimension 1
There are 8 independent parts, one for each index of `af`. A program takes and returns all parts, laid end to end along the dimension named above; an argument that names none is the same for every part. Nothing has to cross between parts.
Inputs may be any that keep to these rules, and one draw needn't show every extreme that they name: Slot s carries the wavenumbers assign[s] and 2047 - assign[s]; every pair appears once.
All inputs are finite; a program needn't handle non-finite values.
Results may differ from a plain program's by a relative error of at most 0.0003.
Values sent between devices are 32-bit elements; how exact they have to be, the bound alone decides.
A program may use at most 64 MiB of HBM per device.

v0:
```python
import jax
import jax.numpy as jnp
from jax import lax
from jax.sharding import PartitionSpec as P

TRUNC = 2047


def synthesize(coeffs, legendre, pair_ids):
    slots = coeffs.shape[0]
    columns = coeffs.shape[1]
    width = coeffs.shape[2]
    entry = lax.broadcasted_iota(jnp.int32, (slots, width), 1)
    first_len = (TRUNC + 1 - pair_ids)[:, None]
    second = entry >= first_len
    degree_gap = jnp.where(second, entry - first_len, entry)
    odd_gap = degree_gap % 2 == 1
    zero_value = jnp.zeros((), coeffs.dtype)
    group_masks = jnp.stack(
        [
            jnp.logical_and(jnp.logical_not(second), jnp.logical_not(odd_gap)),
            jnp.logical_and(jnp.logical_not(second), odd_gap),
            jnp.logical_and(second, jnp.logical_not(odd_gap)),
            jnp.logical_and(second, odd_gap),
        ],
        axis=1,
    )
    masked = jnp.where(group_masks[:, :, None, :], coeffs[:, None, :, :], zero_value)
    masked = masked.reshape(slots, 4 * columns, width)
    partial_value = jnp.einsum("shk,sgk->hgs", legendre, masked, preferred_element_type=jnp.float32)
    lat_half = partial_value.shape[0]
    partial_value = partial_value.reshape(lat_half, 4, columns, slots)
    north_rows = jnp.stack(
        [partial_value[:, 0] + partial_value[:, 1], partial_value[:, 2] + partial_value[:, 3]],
        axis=-1,
    )
    south_rows = jnp.stack(
        [partial_value[:, 0] - partial_value[:, 1], partial_value[:, 2] - partial_value[:, 3]],
        axis=-1,
    )
    north_rows = north_rows.reshape(lat_half, columns, 2 * slots)
    south_rows = south_rows.reshape(lat_half, columns, 2 * slots)
    return jnp.concatenate([north_rows, south_rows[::-1]], axis=0)


def column_places(all_pairs, devices, slots, pieces):
    total = devices * 2 * slots
    half_slots = slots // pieces
    column = jnp.arange(total, dtype=jnp.int32)
    piece_index = column // (devices * 2 * half_slots)
    within_piece = column % (devices * 2 * half_slots)
    source_device = within_piece // (2 * half_slots)
    within = within_piece % (2 * half_slots)
    global_slot = source_device * slots + piece_index * half_slots + within // 2
    owner_pair = jnp.take(all_pairs, global_slot)
    return jnp.where(within % 2 == 0, owner_pair, total - 1 - owner_pair)


def shards(coeffs, legendre, assign):
    devices = lax.axis_size("ma")
    slots = coeffs.shape[0]
    all_pairs = lax.all_gather(assign, "ma", axis=0, tiled=True)
    pieces = 1
    full_rows = synthesize(coeffs, legendre, assign)
    received = lax.all_to_all(full_rows, "ma", split_axis=0, concat_axis=2, tiled=True)
    column_place = column_places(all_pairs, devices, slots, pieces)
    total = received.shape[2]
    source_column = (
        jnp.zeros((total,), jnp.int32).at[column_place].set(jnp.arange(total, dtype=jnp.int32))
    )
    return jnp.take(received, source_column, axis=2)


def solution(mesh):
    return jax.shard_map(
        shards,
        mesh=mesh,
        in_specs=(P("ma", "af", None), P("ma", None, None), P("ma")),
        out_specs=P("ma", "af", None),
        check_vma=False,
    )
```

profile of v0, /device:TPU:1, one launch (start us, length us, event | category | flops | bytes accessed | tf_op | source)
XLA Modules:
  0.0 186.1 jit_solution(17683394474487521863)
XLA Ops:
  0.0 0.7 broadcast_subtract_fusion
  0.7 0.6 not_and_fusion.1
  1.3 0.4 pad_add_fusion
  1.7 2.8 %broadcast_select_fusion = bf16[8,4,64,2049]{3,2,1,0:T(8,128)(2,1)S(1)} fusion(pred[8,4,2049]{2,1,0:T(4,128)(4,1)S(1)} %pad_add_fusion, bf16[8,64,2049]{2,1,0:T(8,128)(2,1)} %param.3), kind=kLoop, calls=%fused_computation.3 | loop fusion | flops 4196352 | bytes 10556448 | tf_op jit(solution)/shard_map/jit(_where)/select_n | solution.py:28
  4.4 6.1 %fusion = f32[8,256,256]{2,1,0:T(8,128)S(1)} fusion(bf16[8,256,2049]{2,1,0:T(8,128)(2,1)S(1)} %bitcast.56, bf16[8,256,2049]{1,0,2:T(8,128)(2,1)} %param.4), kind=kOutput, calls=%fused_computation.4 | convolution fusion | flops 2148532224 | bytes 18882560 | tf_op jit(solution)/shard_map/shk,sgk->hgs/dot_general | solution.py:30
  10.5 0.2 add_bitcast_fusion.1
  10.7 0.1 pad_maximum_fusion.2
  10.8 0.1 copy.41
  10.9 0.5 rev.3
  11.4 0.1 pad_maximum_fusion.1
  11.5 0.3 pad_maximum_fusion
  11.8 3.8 %copy.42 = f32[512,64,16]{1,2,0:T(8,128)} copy(f32[512,64,16]{0,1,2:T(8,128)S(1)} %pad_maximum_fusion) | data formatting | bytes 4194304 | tf_op jit(solution)/shard_map/concatenate | solution.py:43
  15.5 0.0 copy-start.1
  15.5 5.5 %reshape.569 = f32[64,1,8192]{2,1,0:T(1,128)} reshape(f32[512,16,64]{2,1,0:T(8,128)} %bitcast.53) | data formatting | bytes 4194304
  21.0 17.0 %all-to-all-start = ((f32[64,1,8192]{2,1,0:T(1,128)}), f32[64,1,8192]{2,1,0:T(1,128)S(1)}, u32[]{:S(2)}, u32[]{:S(2)}) async-start(f32[64,1,8192]{2,1,0:T(1,128)} %reshape.569), calls=%async_computation | async-start | bytes 4194304 | tf_op jit(solution)/shard_map/all_to_all | solution.py:65
  38.0 1.3 dynamic-slice
  40.1 0.0 copy-done.1
  40.1 0.2 dynamic-update-slice
  40.4 93.4 %all-reduce = s32[512]{0:T(512)S(1)} all-reduce(s32[512]{0:T(512)S(1)} %dynamic-update-slice), channel_id=1, replica_groups=mesh['ma'=64,'af'=8] {'ma'}, use_global_device_ids=true, to_apply=%add | all-reduce | flops 512 | bytes 4096
  133.8 6.9 %gather_fusion = s32[1024]{0:T(1024)S(1)} fusion(s32[512]{0:T(512)S(1)} %all-reduce, s32[1024]{0:T(1024)S(1)} %broadcast_clamp_fusion), kind=kCustom, calls=%fused_computation | custom fusion | bytes 12288 | tf_op jit(solution)/shard_map/jit(_take)/gather | solution.py:55
  140.8 4.5 %scatter_custom_fusion = s32[1024]{0:T(1024)S(1)} fusion(s32[1024]{0:T(1024)S(1)} %bitcast.62, s32[1024]{0:T(1024)S(1)} %iota.27, s32[]{:T(128)} %constant.100.clone.1), kind=kCustom, calls=%fused_computation.53 | custom fusion | bytes 4100 | tf_op jit(solution)/shard_map/scatter | solution.py:69
  145.3 0.0 all-to-all-done
  145.3 0.0 copy-start
  145.3 1.3 copy-done
  146.6 0.6 broadcast.789
  147.2 7.6 %reduce = f32[64,8192]{1,0:T(8,128)S(1)} reduce(f32[64,1,8192]{2,1,0:T(1,128)} %copy-done, f32[]{:T(128)} %broadcast.789), dimensions={1}, to_apply=%all_to_all.13.reduce_sub_computation | reduce | bytes 4194308 | tf_op jit(solution)/shard_map/all_to_all | solution.py:65
  154.8 3.0 %reshape.570 = f32[512,16,64]{2,1,0:T(8,128)} reshape(f32[64,8192]{1,0:T(8,128)S(1)} %reduce) | data formatting | bytes 4194304
  157.8 2.6 %copy.43 = f32[8,64,64,16]{1,3,2,0:T(8,128)S(1)} copy(f32[8,64,64,16]{1,3,0,2:T(8,128)} %bitcast.54) | data formatting | bytes 4194304 | tf_op jit(solution)/shard_map/all_to_all | solution.py:65
  160.4 4.4 %copy.44 = f32[8,64,1024]{1,0,2:T(8,128)} copy(f32[8,64,1024]{1,2,0:T(8,128)S(1)} %bitcast.55) | data formatting | bytes 4194304 | tf_op jit(solution)/shard_map/all_to_all | solution.py:65
  164.8 10.4 %gather_fusion.1 = f32[1024,8,64]{2,1,0:T(8,128)} fusion(f32[8,64,1024]{1,0,2:T(8,128)} %copy.44, s32[1024]{0:T(1024)S(1)} %fusion.6), kind=kCustom, calls=%fused_computation.1 | custom fusion | bytes 4198400 | tf_op jit(solution)/shard_map/jit(_take)/gather | solution.py:71
  175.1 7.2 %select_bitcast_fusion = f32[8,64,1024]{1,0,2:T(8,128)} fusion(f32[1024,8,64]{2,1,0:T(8,128)} %gather_fusion.1, pred[1024]{0:T(1024)(128)(4,1)S(1)} %compare_and_fusion), kind=kLoop, calls=%fused_computation.6 | loop fusion | flops 524288 | bytes 4195328 | tf_op jit(solution)/shard_map/jit(_take)/select_n | solution.py:71
  182.3 3.8 %copy.45 = f32[8,64,1024]{2,1,0:T(8,128)} copy(f32[8,64,1024]{1,0,2:T(8,128)} %select_bitcast_fusion) | data formatting | bytes 4194304 | tf_op jit(solution)/shard_map/jit(_take)/select_n | solution.py:71
  (7 shorter events, 0.1 us)
Async XLA Ops:
  15.5 24.6 %copy-start.1 = (s32[8]{0:T(128)S(1)}, s32[8]{0:T(128)}, u32[]{:S(2)}) copy-start(s32[8]{0:T(128)} %param.5) | copy-start | bytes 100
  21.0 124.3 %all-to-all-start = ((f32[64,1,8192]{2,1,0:T(1,128)}), f32[64,1,8192]{2,1,0:T(1,128)S(1)}, u32[]{:S(2)}, u32[]{:S(2)}) async-start(f32[64,1,8192]{2,1,0:T(1,128)} %reshape.569), calls=%async_computation | async-start | bytes 4194304 | tf_op jit(solution)/shard_map/all_to_all | solution.py:65
  145.3 1.3 copy-start
where the time goes:
time: 187 us; the launch traced here: 186 us
  blocking collectives  93.4 us (50%)
  local copies, waits for them, and re-layouts  48.8 us (26%)
  other arithmetic  19.9 us (11%)
  starting transfers between devices  17 us (9%)
  matrix products  6.07 us (3%)
    unnamed x1, blocking collectives  93.4 us
    all_to_all x1, starting transfers between devices, shards(): lax.all_to_all(full_rows, 'ma', split_axis=0, concat_axis=2, tiled=True)  17 us
    unnamed x9, local copies, waits for them, and re-layouts  11.4 us
    gather x1, local copies, waits for them, and re-layouts, shards(): return jnp.take(received, source_column, axis=2)  10.4 us
    all_to_all x1, other arithmetic, shards(): lax.all_to_all(full_rows, 'ma', split_axis=0, concat_axis=2, tiled=True)  7.58 us
    all_to_all x3, local copies, waits for them, and re-layouts, shards(): lax.all_to_all(full_rows, 'ma', split_axis=0, concat_axis=2, tiled=True)  7.53 us
    select_n x1, other arithmetic, shards(): return jnp.take(received, source_column, axis=2)  7.15 us
    gather x1, local copies, waits for them, and re-layouts, column_places(): owner_pair = jnp.take(all_pairs, global_slot)  6.87 us
  transfers between devices with their start and end apart: 1, of which 0 were waited for; matrix products, arithmetic and copies ran while one was open for 7% of the time, Pallas kernels for 0%

commit v1 on v0

v1 whole, which is shorter than its diff:
```python
import jax
import jax.numpy as jnp
from jax import lax
from jax.experimental import pallas as pl
from jax.experimental.pallas import tpu as pltpu
from jax.sharding import PartitionSpec as P

TRUNC = 2047
MESH = pl.DeviceIdType.MESH
N = 64
SLOTS = 8
HLAT = 256
COLS = 64
KMAIN = 2048
CHUNK = 256
F32 = jnp.float32
BF16 = jnp.bfloat16
I32 = jnp.int32


def other(me, t):
    out = 0
    for b in range(6):
        bit = lax.rem(lax.div(me, 1 << b) + lax.div(t, 1 << b), 2)
        out = out + bit * (1 << b)
    return out


def place_of(d):
    south = lax.div(d, 32)
    return d + south * (95 - 2 * d)


def kernel(
    assign_hbm, coeffs_hbm, legendre_hbm, out_ref,
    pair_smem, coeffs_v, raw_v, leg_v, signed_v, send, recv, my_row, rows, vals, hot,
    pair_sem, coeffs_sem, leg_sem, send_sem, recv_sem, row_send_sem, row_recv_sem,
):
    me = lax.axis_index("ma")
    z = lax.div(me, 8)
    zhalf = lax.div(z, 4)

    pair_copy = pltpu.make_async_copy(assign_hbm, pair_smem, pair_sem)
    pair_copy.start()
    coeffs_copy = pltpu.make_async_copy(coeffs_hbm, coeffs_v, coeffs_sem)
    coeffs_copy.start()

    def leg_copy(i):
        rows_of = pl.ds(i * CHUNK, CHUNK)
        return pltpu.make_async_copy(legendre_hbm.at[rows_of], raw_v.at[rows_of], leg_sem.at[i])

    chunks = KMAIN // CHUNK
    for i in range(chunks):
        leg_copy(i).start()
    tail_copy = pltpu.make_async_copy(
        legendre_hbm.at[pl.ds(KMAIN, 1)], raw_v.at[pl.ds(KMAIN, 1)], leg_sem.at[chunks]
    )
    tail_copy.start()

    barrier = pltpu.get_barrier_semaphore()

    def greet(t, carry):
        a = lax.div(t, 8)
        plane = a * zhalf + (7 - a) * (1 - zhalf)
        d = plane * 8 + lax.rem(t, 8)
        pl.semaphore_signal(barrier, inc=1, device_id={"ma": d}, device_id_type=MESH)
        return carry

    lax.fori_loop(0, N, greet, 0)

    pair_copy.wait()
    lane = lax.broadcasted_iota(I32, (1, 128), 1)
    first_lane = lax.rem(me, 16) * SLOTS
    row = jnp.zeros((1, 128), I32)
    for s in range(SLOTS):
        row = jnp.where(lane == first_lane + s, pair_smem[s], row)
    my_row[0] = row
    rows[me] = row

    def regroup(i, carry):
        leg_copy(i).wait()
        for j in range(CHUNK // 32):
            start = pl.multiple_of(i * CHUNK + j * 32, 32)
            leg_v[:, pl.ds(start, 32), :] = jnp.transpose(raw_v[pl.ds(start, 32)], (1, 0, 2))
        return carry

    lax.fori_loop(0, chunks, regroup, 0)
    tail_copy.wait()
    coeffs_copy.wait()
    last_row = raw_v[KMAIN].astype(F32)
    slot_of = lax.broadcasted_iota(I32, (SLOTS, HLAT), 0)
    entry = lax.broadcasted_iota(I32, (1, KMAIN), 1)

    def one_slot(s, carry):
        pair = pair_smem[s]
        first_len = TRUNC + 1 - pair
        second = entry >= first_len
        sign_first = 1 - 2 * (entry & 1)
        sign_second = 1 - 2 * ((entry - first_len) & 1)
        c = coeffs_v[s, :, 0:KMAIN]
        masks = (
            jnp.where(second, 0, 1),
            jnp.where(second, 1, 0),
            jnp.where(second, 0, sign_first),
            jnp.where(second, sign_second, 0),
        )
        for g, mask in enumerate(masks):
            signed_v[g * COLS:(g + 1) * COLS, :] = c * mask.astype(F32).astype(BF16)
        part = jnp.dot(signed_v[...], leg_v[s], preferred_element_type=F32)
        leg_row = jnp.sum(jnp.where(slot_of == s, last_row, 0.0), axis=0, keepdims=True)
        edge = coeffs_v[s, :, KMAIN:KMAIN + 1].astype(F32) * leg_row
        edge_sign = (1 - 2 * (pair & 1)).astype(F32)
        north = jnp.concatenate([part[0:COLS], part[COLS:2 * COLS] + edge], axis=0)
        south = jnp.concatenate(
            [part[2 * COLS:3 * COLS], part[3 * COLS:4 * COLS] + edge * edge_sign], axis=0
        )
        mine = pl.ds(pl.multiple_of(s * 8, 8), 8)
        send[0:32, mine, :] = north.T.reshape(32, 8, 128)
        send[32:64, mine, :] = south.T.reshape(32, 8, 128)
        return carry

    lax.fori_loop(0, SLOTS, one_slot, 0)

    def block_copy(t):
        d = other(me, t)
        return pltpu.make_async_remote_copy(
            src_ref=send.at[place_of(d)], dst_ref=recv.at[me], send_sem=send_sem.at[t], recv_sem=recv_sem.at[me],
            device_id={"ma": d}, device_id_type=MESH,
        )

    def row_copy(t):
        return pltpu.make_async_remote_copy(
            src_ref=my_row.at[0], dst_ref=rows.at[me], send_sem=row_send_sem.at[t], recv_sem=row_recv_sem.at[me],
            device_id={"ma": other(me, t)}, device_id_type=MESH,
        )

    pl.semaphore_wait(barrier, N)

    def send_row(t, carry):
        row_copy(t).start()
        return carry

    def send_block(t, carry):
        block_copy(t).start()
        return carry

    lax.fori_loop(1, N, send_row, 0)
    lax.fori_loop(1, N, send_block, 0)
    recv[me] = send[place_of(me)]

    out_ref[...] = jnp.zeros_like(out_ref)
    half = lax.div(me, 32)
    column = lax.broadcasted_iota(I32, (512, 128), 0)

    def one_group(step, carry):
        late = lax.div(step, 2)
        second = lax.rem(step, 2)
        group = (1 - late) * (2 * zhalf + second) + late * (3 * (1 - zhalf) * (1 - second) + (2 - zhalf) * second)

        def arrived(i, c):
            src = group * 16 + i

            @pl.when(src != me)
            def _():
                pltpu.make_async_copy(rows.at[src], rows.at[src], row_recv_sem.at[src]).wait()
                pltpu.make_async_copy(recv.at[src], recv.at[src], recv_sem.at[src]).wait()

            return c

        lax.fori_loop(0, 16, arrived, 0)
        pairs = jnp.sum(rows[pl.ds(group * 16, 16)], axis=0)
        first_hot = jnp.where(column == pairs, 1.0, 0.0).astype(BF16)
        second_hot = jnp.where(column == 511 - pairs, 1.0, 0.0).astype(BF16)
        hot[0, :, 0:128] = first_hot
        hot[0, :, 128:256] = first_hot
        hot[1, :, 0:128] = second_hot
        hot[1, :, 128:256] = second_hot
        for i in range(8):
            r = i + half * (7 - 2 * i)
            got = jnp.concatenate(
                [recv[group * 16 + j, pl.ds(r, 8, stride=8), :] for j in range(16)], axis=0
            ).T
            high = got.astype(BF16)
            low = (got - high.astype(F32)).astype(BF16)
            for w in range(2):
                vals[w, i * COLS:(i + 1) * COLS, 0:128] = high[w * COLS:(w + 1) * COLS]
                vals[w, i * COLS:(i + 1) * COLS, 128:256] = low[w * COLS:(w + 1) * COLS]
        for w in range(2):
            out_ref[:, w * 512:(w + 1) * 512] += lax.dot_general(
                vals[w], hot[w], (((1,), (1,)), ((), ())), preferred_element_type=F32
            )
        return carry

    lax.fori_loop(0, 4, one_group, 0)

    def sent(t, carry):
        row_copy(t).wait_send()
        block_copy(t).wait_send()
        return carry

    lax.fori_loop(1, N, sent, 0)


def shards(coeffs, legendre, assign):
    leg = jnp.transpose(legendre, (2, 0, 1))
    dma = pltpu.SemaphoreType.DMA
    out = pl.pallas_call(
        kernel,
        name="synthesis",
        out_shape=jax.ShapeDtypeStruct((512, 1024), F32),
        in_specs=[pl.BlockSpec(memory_space=pltpu.HBM)] * 3,
        out_specs=pl.BlockSpec(memory_space=pltpu.VMEM),
        scratch_shapes=[
            pltpu.SMEM((SLOTS,), I32),
            pltpu.VMEM((SLOTS, COLS, KMAIN + 1), BF16),
            pltpu.VMEM((KMAIN + 1, SLOTS, HLAT), BF16),
            pltpu.VMEM((SLOTS, KMAIN, HLAT), BF16),
            pltpu.VMEM((4 * COLS, KMAIN), BF16),
            pltpu.VMEM((N, 64, 128), F32),
            pltpu.VMEM((N, 64, 128), F32),
            pltpu.VMEM((1, 1, 128), I32),
            pltpu.VMEM((N, 1, 128), I32),
            pltpu.VMEM((2, 512, 256), BF16),
            pltpu.VMEM((2, 512, 256), BF16),
            dma,
            dma,
            dma((KMAIN // CHUNK + 1,)),
            dma((N,)),
            dma((N,)),
            dma((N,)),
            dma((N,)),
        ],
        compiler_params=pltpu.CompilerParams(
            collective_id=0, has_side_effects=True, vmem_limit_bytes=44 * 2**20
        ),
    )(assign, coeffs, leg)
    return out.reshape(8, COLS, 1024)


def solution(mesh):
    return jax.shard_map(
        shards,
        mesh=mesh,
        in_specs=(P("ma", "af", None), P("ma", None, None), P("ma")),
        out_specs=P("ma", "af", None),
        check_vma=False,
    )
```

time: 187 us -> 116 us (0.62)
  the two profiles are of different devices: /device:TPU:1 before, /device:TPU:97 now
where the time goes in v1:
time: 116 us
  Pallas kernels  112 us (97%)
  local copies, waits for them, and re-layouts  3.6 us (3%)
    pallas_call x1, Pallas kernels, shards(): pl.pallas_call(kernel, name='synthesis', out_shape=jax.ShapeDtypeStruct((...  112 us
    unnamed x5, local copies, waits for them, and re-layouts  3.6 us

profile of v1, /device:TPU:97, one launch (start us, length us, event | category | flops | bytes accessed | tf_op | source)
XLA Modules:
  0.0 116.0 jit_solution(727106955376651883)
XLA Ops:
  0.0 0.0 copy-start
  0.0 1.6 %copy-done = bf16[8,64,2049]{2,1,0:T(8,128)(2,1)S(1)} copy-done((bf16[8,64,2049]{2,1,0:T(8,128)(2,1)S(1)}, bf16[8,64,2049]{2,1,0:T(8,128)(2,1)}, u32[]{:S(2)}) %copy-start) | copy-done | bytes 2098200
  1.6 0.0 copy-start.1
  1.6 0.7 copy-done.1
  2.3 112.4 %synthesis.1 = f32[512,1024]{1,0:T(8,128)S(1)} custom-call(s32[8]{0:T(128)S(1)} %copy-done.1, bf16[8,64,2049]{2,1,0:T(8,128)(2,1)S(1)} %copy-done, bf16[2049,8,256]{2,1,0:T(8,128)(2,1)} %bitcast.3), custom_call_target="tpu_custom_call" | custom-call | tf_op jit(solution)/shard_map/synthesis/pallas_call | solution.py:207
  114.7 1.3 %copy.5 = f32[8,64,1024]{2,1,0:T(8,128)} copy(f32[8,64,1024]{2,1,0:T(8,128)S(1)} %bitcast.2) | data formatting | bytes 4194304
Async XLA Ops:
  0.0 1.6 %copy-start = (bf16[8,64,2049]{2,1,0:T(8,128)(2,1)S(1)}, bf16[8,64,2049]{2,1,0:T(8,128)(2,1)}, u32[]{:S(2)}) copy-start(bf16[8,64,2049]{2,1,0:T(8,128)(2,1)} %coeffs_hbm.1) | copy-start | bytes 6294532
  1.6 0.7 copy-start.1

commit v2 on v1

v2 whole, which is shorter than its diff:
```python
import jax
import jax.numpy as jnp
from jax import lax
from jax.experimental import pallas as pl
from jax.experimental.pallas import tpu as pltpu
from jax.sharding import PartitionSpec as P

TRUNC = 2047
MESH = pl.DeviceIdType.MESH
N = 64
SLOTS = 8
HLAT = 256
COLS = 64
KMAIN = 2048
CUTS = (0, 1024, 2048)
CHUNKS = len(CUTS) - 1
CHUNK = max(b - a for a, b in zip(CUTS, CUTS[1:]))
F32 = jnp.float32
BF16 = jnp.bfloat16
I32 = jnp.int32


def other(me, t, bits):
    out = 0
    for b in range(bits):
        bit = lax.rem(lax.div(me, 1 << b) + lax.div(t, 1 << b), 2)
        out = out + bit * (1 << b)
    return out


def place_of(d):
    south = lax.div(d, 32)
    return d + south * (95 - 2 * d)


def kernel(
    assign_hbm, coeffs_hbm, legendre_hbm, out_ref,
    pair_smem, coeffs_v, raw_v, leg_v, signed_v, acc, send, recv, my_row, rows, plane_row, plane_rows, vals, hot,
    ready, pair_sem, coeffs_sem, leg_sem, send_sem, recv_sem,
    row_send_sem, row_recv_sem, plane_send_sem, plane_recv_sem,
):
    me = lax.axis_index("ma")
    z = lax.div(me, 8)
    here = lax.rem(me, 8)
    zhalf = lax.div(z, 4)

    pair_copy = pltpu.make_async_copy(assign_hbm, pair_smem, pair_sem)
    pair_copy.start()
    coeffs_copy = pltpu.make_async_copy(coeffs_hbm, coeffs_v, coeffs_sem)
    coeffs_copy.start()

    def leg_copy(i):
        rows_of = pl.ds(CUTS[i], CUTS[i + 1] - CUTS[i] + i // (CHUNKS - 1))
        return pltpu.make_async_copy(legendre_hbm.at[rows_of], raw_v.at[rows_of], leg_sem.at[i])

    for i in range(CHUNKS):
        leg_copy(i).start()

    barrier = pltpu.get_barrier_semaphore()
    for plane in reversed(range(8)):
        @pl.when(plane >= z)
        def _():
            for b in range(8):
                pl.semaphore_signal(barrier, inc=1, device_id={"ma": plane * 8 + b}, device_id_type=MESH)

    pair_copy.wait()
    lane = lax.broadcasted_iota(I32, (1, 128), 1)
    first_lane = lax.rem(me, 16) * SLOTS
    row = jnp.zeros((1, 128), I32)
    for s in range(SLOTS):
        row = jnp.where(lane == first_lane + s, pair_smem[s], row)
    my_row[0] = row
    rows[here] = row

    pl.semaphore_wait(barrier, 8 * (z + 1))
    for plane in range(7):
        @pl.when(plane < z)
        def _():
            for b in range(8):
                pl.semaphore_signal(ready.at[z], inc=1, device_id={"ma": plane * 8 + b}, device_id_type=MESH)

    def row_copy(b):
        return pltpu.make_async_remote_copy(
            src_ref=my_row.at[0], dst_ref=rows.at[here], send_sem=row_send_sem.at[b], recv_sem=row_recv_sem.at[here],
            device_id={"ma": z * 8 + b}, device_id_type=MESH,
        )

    def plane_copy(plane):
        return pltpu.make_async_remote_copy(
            src_ref=plane_row.at[0], dst_ref=plane_rows.at[z], send_sem=plane_send_sem.at[plane],
            recv_sem=plane_recv_sem.at[z], device_id={"ma": plane * 8 + here}, device_id_type=MESH,
        )

    def mates(body):
        for b in range(8):
            @pl.when(b != here)
            def _():
                body(b)

    def planes(body):
        for plane in range(8):
            @pl.when(plane != z)
            def _():
                body(plane)

    mates(lambda b: row_copy(b).start())

    coeffs_copy.wait()
    entry = lax.broadcasted_iota(I32, (1, KMAIN), 1)

    def sign(s, carry):
        first_len = TRUNC + 1 - pair_smem[s]
        second = entry >= first_len
        sign_first = 1 - 2 * (entry & 1)
        sign_second = 1 - 2 * ((entry - first_len) & 1)
        c = coeffs_v[s, :, 0:KMAIN]
        masks = (
            jnp.where(second, 0, 1),
            jnp.where(second, 1, 0),
            jnp.where(second, 0, sign_first),
            jnp.where(second, sign_second, 0),
        )
        for g, mask in enumerate(masks):
            signed_v[s, g * COLS:(g + 1) * COLS, :] = c * mask.astype(F32).astype(BF16)
        return carry

    lax.fori_loop(0, SLOTS, sign, 0)

    slot_of = lax.broadcasted_iota(I32, (SLOTS, HLAT), 0)

    def synthesize():
        for i in range(CHUNKS):
            leg_copy(i).wait()
            size = CUTS[i + 1] - CUTS[i]
            for j in range(0, size, 32):
                leg_v[:, j:j + 32, :] = jnp.transpose(raw_v[CUTS[i] + j:CUTS[i] + j + 32], (1, 0, 2))

            def add(s, carry, i=i, size=size):
                here = jnp.dot(
                    signed_v[s, :, CUTS[i]:CUTS[i + 1]], leg_v[s, 0:size], preferred_element_type=F32
                )
                if i == 0:
                    acc[s] = here
                else:
                    acc[s] += here
                return carry

            if i < CHUNKS - 1:
                lax.fori_loop(0, SLOTS, add, 0, unroll=True)

        def finish(s, carry):
            i = CHUNKS - 1
            size = CUTS[i + 1] - CUTS[i]
            total = acc[s] + jnp.dot(
                signed_v[s, :, CUTS[i]:CUTS[i + 1]], leg_v[s, 0:size], preferred_element_type=F32
            )
            last = raw_v[KMAIN].astype(F32)
            last = jnp.sum(jnp.where(slot_of == s, last, 0.0), axis=0, keepdims=True)
            edge = coeffs_v[s, :, KMAIN:KMAIN + 1].astype(F32) * last
            edge_sign = (1 - 2 * (pair_smem[s] & 1)).astype(F32)
            north = jnp.concatenate([total[0:COLS], total[COLS:2 * COLS] + edge], axis=0)
            south = jnp.concatenate(
                [total[2 * COLS:3 * COLS], total[3 * COLS:4 * COLS] + edge * edge_sign], axis=0
            )
            mine = pl.ds(pl.multiple_of(s * 8, 8), 8)
            send[0:32, mine, :] = north.T.reshape(32, 8, 128)
            send[32:64, mine, :] = south.T.reshape(32, 8, 128)
            return carry

        lax.fori_loop(0, SLOTS, finish, 0, unroll=True)

    def block_copy(d):
        return pltpu.make_async_remote_copy(
            src_ref=send.at[place_of(d)], dst_ref=recv.at[me], send_sem=send_sem.at[d], recv_sem=recv_sem.at[me],
            device_id={"ma": d}, device_id_type=MESH,
        )

    synthesize()

    mates(lambda b: pltpu.make_async_copy(rows.at[b], rows.at[b], row_recv_sem.at[b]).wait())
    pairs_here = jnp.sum(rows[...], axis=0)
    plane_row[0] = pairs_here
    plane_rows[z] = pairs_here


    for plane in range(1, 8):
        @pl.when(plane > z)
        def _():
            pl.semaphore_wait(ready.at[plane], 8)

    planes(lambda plane: plane_copy(plane).start())

    def send_rest(t, carry):
        d = other(me, lax.div(t, 2) + 32 * (1 - lax.rem(t, 2)), 6)

        @pl.when(d != me)
        def _():
            block_copy(d).start()

        return carry

    lax.fori_loop(0, N, send_rest, 0)
    recv[me] = send[place_of(me)]
    planes(lambda plane: pltpu.make_async_copy(plane_rows.at[plane], plane_rows.at[plane], plane_recv_sem.at[plane]).wait())

    out_ref[...] = jnp.zeros_like(out_ref)
    half = lax.div(me, 32)
    column = lax.broadcasted_iota(I32, (512, 128), 0)

    def one_group(step, carry):
        late = lax.div(step, 2)
        second = lax.rem(step, 2)
        group = (1 - late) * (2 * zhalf + second) + late * (3 * (1 - zhalf) * (1 - second) + (2 - zhalf) * second)

        def arrived(i, c):
            src = group * 16 + i
            @pl.when(src != me)
            def _():
                pltpu.make_async_copy(recv.at[src], recv.at[src], recv_sem.at[src]).wait()

            return c

        lax.fori_loop(0, 16, arrived, 0)
        pairs = plane_rows[2 * group] + plane_rows[2 * group + 1]
        first_hot = jnp.where(column == pairs, 1.0, 0.0).astype(BF16)
        second_hot = jnp.where(column == 511 - pairs, 1.0, 0.0).astype(BF16)
        hot[0, :, 0:128] = first_hot
        hot[0, :, 128:256] = first_hot
        hot[1, :, 0:128] = second_hot
        hot[1, :, 128:256] = second_hot
        for i in range(8):
            r = i + half * (7 - 2 * i)
            got = jnp.concatenate(
                [recv[group * 16 + j, pl.ds(r, 8, stride=8), :] for j in range(16)], axis=0
            ).T
            high = got.astype(BF16)
            low = (got - high.astype(F32)).astype(BF16)
            for w in range(2):
                vals[w, i * COLS:(i + 1) * COLS, 0:128] = high[w * COLS:(w + 1) * COLS]
                vals[w, i * COLS:(i + 1) * COLS, 128:256] = low[w * COLS:(w + 1) * COLS]
        for w in range(2):
            out_ref[:, w * 512:(w + 1) * 512] += lax.dot_general(
                vals[w], hot[w], (((1,), (1,)), ((), ())), preferred_element_type=F32
            )
        return carry

    lax.fori_loop(0, 4, one_group, 0)

    mates(lambda b: row_copy(b).wait_send())
    planes(lambda plane: plane_copy(plane).wait_send())

    def sent(d, carry):
        @pl.when(d != me)
        def _():
            block_copy(d).wait_send()

        return carry

    lax.fori_loop(0, N, sent, 0)


def shards(coeffs, legendre, assign):
    leg = jnp.transpose(legendre, (2, 0, 1))
    dma = pltpu.SemaphoreType.DMA
    out = pl.pallas_call(
        kernel,
        name="synthesis",
        out_shape=jax.ShapeDtypeStruct((512, 1024), F32),
        in_specs=[pl.BlockSpec(memory_space=pltpu.HBM)] * 3,
        out_specs=pl.BlockSpec(memory_space=pltpu.VMEM),
        scratch_shapes=[
            pltpu.SMEM((SLOTS,), I32),
            pltpu.VMEM((SLOTS, COLS, KMAIN + 1), BF16),
            pltpu.VMEM((KMAIN + 1, SLOTS, HLAT), BF16),
            pltpu.VMEM((SLOTS, CHUNK, HLAT), BF16),
            pltpu.VMEM((SLOTS, 4 * COLS, KMAIN), BF16),
            pltpu.VMEM((SLOTS, 4 * COLS, HLAT), F32),
            pltpu.VMEM((N, 64, 128), F32),
            pltpu.VMEM((N, 64, 128), F32),
            pltpu.VMEM((1, 1, 128), I32),
            pltpu.VMEM((8, 1, 128), I32),
            pltpu.VMEM((1, 1, 128), I32),
            pltpu.VMEM((8, 1, 128), I32),
            pltpu.VMEM((2, 512, 256), BF16),
            pltpu.VMEM((2, 512, 256), BF16),
            pltpu.SemaphoreType.REGULAR((8,)),
            dma,
            dma,
            dma((CHUNKS,)),
            dma((N,)),
            dma((N,)),
            dma((8,)),
            dma((8,)),
            dma((8,)),
            dma((8,)),
        ],
        compiler_params=pltpu.CompilerParams(
            collective_id=0, has_side_effects=True, vmem_limit_bytes=44 * 2**20
        ),
    )(*(pltpu.with_memory_space_constraint(x, pltpu.HBM) for x in (assign, coeffs, leg)))
    return out.reshape(8, COLS, 1024)


def solution(mesh):
    return jax.shard_map(
        shards,
        mesh=mesh,
        in_specs=(P("ma", "af", None), P("ma", None, None), P("ma")),
        out_specs=P("ma", "af", None),
        check_vma=False,
    )
```

time: 116 us -> 110 us (0.948)
  Pallas kernels: 112 us -> 109 us
  local copies, waits for them, and re-layouts: 3.6 us -> 1.32 us
    pallas_call x1, Pallas kernels: 112 us -> 109 us  [shards(): pl.pallas_call(kernel, name='synthesis', out_shape=jax.ShapeDtypeStruct((...]
    unnamed x5 -> x1, local copies, waits for them, and re-layouts: 3.6 us -> 1.32 us
where the time goes in v2:
time: 110 us
  Pallas kernels  109 us (99%)
  local copies, waits for them, and re-layouts  1.32 us (1%)
    pallas_call x1, Pallas kernels, shards(): pl.pallas_call(kernel, name='synthesis', out_shape=jax.ShapeDtypeStruct((...  109 us

profile of v2, /device:TPU:97, one launch (start us, length us, event | category | flops | bytes accessed | tf_op | source)
XLA Modules:
  0.0 110.2 jit_solution(2815586934152332281)
XLA Ops:
  0.0 108.9 %synthesis.1 = f32[512,1024]{1,0:T(8,128)S(1)} custom-call(s32[8]{0:T(128)} %assign_hbm.1, bf16[8,64,2049]{2,1,0:T(8,128)(2,1)} %coeffs_hbm.1, bf16[2049,8,256]{2,1,0:T(8,128)(2,1)} %bitcast.3), custom_call_target="tpu_custom_call" | custom-call | tf_op jit(solution)/shard_map/synthesis/pallas_call | solution.py:265
  108.9 1.3 %copy.5 = f32[8,64,1024]{2,1,0:T(8,128)} copy(f32[8,64,1024]{2,1,0:T(8,128)S(1)} %bitcast.2) | data formatting | bytes 4194304

commit v3 on v2

--- a/solution.py
+++ b/solution.py
@@ -12,7 +12,7 @@
 HLAT = 256
 COLS = 64
 KMAIN = 2048
-CUTS = (0, 1024, 2048)
+CUTS = (0, 1280, 2048)
 CHUNKS = len(CUTS) - 1
 CHUNK = max(b - a for a, b in zip(CUTS, CUTS[1:]))
 F32 = jnp.float32
@@ -184,14 +184,27 @@
 
 
     for plane in range(1, 8):
-        @pl.when(plane > z)
+        @pl.when(jnp.logical_and(plane > z, zhalf == plane // 4))
         def _():
             pl.semaphore_wait(ready.at[plane], 8)
 
-    planes(lambda plane: plane_copy(plane).start())
-
-    def send_rest(t, carry):
-        d = other(me, lax.div(t, 2) + 32 * (1 - lax.rem(t, 2)), 6)
+
+    for plane in range(8):
+        @pl.when(jnp.logical_and(plane != z, plane < 4 * (zhalf + 1)))
+        def _():
+            plane_copy(plane).start()
+
+    def send_pair(t, carry):
+        e = lax.div(t, 8)
+        plane = other(z, 4 + e + (1 - zhalf) * (4 * (1 - lax.min(e, 1)) - 1), 3)
+
+        @pl.when(jnp.logical_and(lax.rem(t, 8) == 0, zhalf == 0))
+        def _():
+            pl.semaphore_wait(ready.at[plane], 8)
+            plane_copy(plane).start()
+
+        block_copy(plane * 8 + other(here, lax.rem(t, 8), 3)).start()
+        d = other(me, t, 5) + 32 * zhalf
 
         @pl.when(d != me)
         def _():
@@ -199,13 +212,20 @@
 
         return carry
 
-    lax.fori_loop(0, N, send_rest, 0)
+    lax.fori_loop(0, N // 2, send_pair, 0)
     recv[me] = send[place_of(me)]
     planes(lambda plane: pltpu.make_async_copy(plane_rows.at[plane], plane_rows.at[plane], plane_recv_sem.at[plane]).wait())
 
     out_ref[...] = jnp.zeros_like(out_ref)
     half = lax.div(me, 32)
     column = lax.broadcasted_iota(I32, (512, 128), 0)
+
+    def sent(d, carry):
+        @pl.when(d != me)
+        def _():
+            block_copy(d).wait_send()
+
+        return carry
 
     def one_group(step, carry):
         late = lax.div(step, 2)
@@ -220,7 +240,6 @@
 
             return c
 
-        lax.fori_loop(0, 16, arrived, 0)
         pairs = plane_rows[2 * group] + plane_rows[2 * group + 1]
         first_hot = jnp.where(column == pairs, 1.0, 0.0).astype(BF16)
         second_hot = jnp.where(column == 511 - pairs, 1.0, 0.0).astype(BF16)
@@ -228,6 +247,14 @@
         hot[0, :, 128:256] = first_hot
         hot[1, :, 0:128] = second_hot
         hot[1, :, 128:256] = second_hot
+
+        @pl.when(step == 3)
+        def _():
+            mates(lambda b: row_copy(b).wait_send())
+            planes(lambda plane: plane_copy(plane).wait_send())
+            lax.fori_loop(0, N, sent, 0)
+
+        lax.fori_loop(0, 16, arrived, 0)
         for i in range(8):
             r = i + half * (7 - 2 * i)
             got = jnp.concatenate(
@@ -245,18 +272,6 @@
         return carry
 
     lax.fori_loop(0, 4, one_group, 0)
-
-    mates(lambda b: row_copy(b).wait_send())
-    planes(lambda plane: plane_copy(plane).wait_send())
-
-    def sent(d, carry):
-        @pl.when(d != me)
-        def _():
-            block_copy(d).wait_send()
-
-        return carry
-
-    lax.fori_loop(0, N, sent, 0)
 
 
 def shards(coeffs, legendre, assign):

time: 110 us -> 110 us (level)
  no operation moved by 1% of the time
where the time goes in v3:
time: 110 us
  Pallas kernels  108 us (98%)
  local copies, waits for them, and re-layouts  1.32 us (1%)
    pallas_call x1, Pallas kernels, shards(): pl.pallas_call(kernel, name='synthesis', out_shape=jax.ShapeDtypeStruct((...  108 us

profile of v3, /device:TPU:97, one launch (start us, length us, event | category | flops | bytes accessed | tf_op | source)
XLA Modules:
  0.0 109.7 jit_solution(15674603135054573104)
XLA Ops:
  0.0 108.4 %synthesis.1 = f32[512,1024]{1,0:T(8,128)S(1)} custom-call(s32[8]{0:T(128)} %assign_hbm.1, bf16[8,64,2049]{2,1,0:T(8,128)(2,1)} %coeffs_hbm.1, bf16[2049,8,256]{2,1,0:T(8,128)(2,1)} %bitcast.3), custom_call_target="tpu_custom_call" | custom-call | tf_op jit(solution)/shard_map/synthesis/pallas_call | solution.py:280
  108.4 1.3 %copy.5 = f32[8,64,1024]{2,1,0:T(8,128)} copy(f32[8,64,1024]{2,1,0:T(8,128)S(1)} %bitcast.2) | data formatting | bytes 4194304
